TPU v7x, 32 devices: a whole 2x2x4 slice. The times are simulated.
32 devices in a mesh: groups: 2 (over x), steps: 8 (over z, y), inner: 2 (over core).
Axes of the slice: x: 2, y: 2, z: 4, core: 2. Of those that a mesh axis runs over, the one named last changes fastest.
Arguments:
- start_state: float32 [16, 32, 768], P('groups'), parts along dimension 0, may hold values from -6 to 6
- noise_draws: float32 [32, 8, 32, 768], P(('groups', 'steps', 'inner')), parts along dimension 0, may hold values from -6 to 6
- step_gaps: int32 [32], P(('groups', 'steps', 'inner')), parts along dimension 0, may hold values from 1 to 15
- window_start: int32 [2], P('groups'), parts along dimension 0, may hold values from 240 to 999
- input_weight: bfloat16 [768, 1024], replicated, may hold values from -0.21875 to 0.21875
- embed_weight: bfloat16 [256, 2048], replicated, may hold values from -0.375 to 0.375
- first_weight: bfloat16 [1024, 1024], replicated, may hold values from -0.1875 to 0.1875
- second_weight: bfloat16 [1024, 1024], replicated, may hold values from -0.1875 to 0.1875
- output_weight: bfloat16 [1024, 768], replicated, may hold values from -0.1875 to 0.1875
Outputs:
- trajectory: float32 [32, 8, 32, 768], P(('groups', 'steps', 'inner')), parts along dimension 0
There are 2 independent parts, one for each index of `groups`. A program takes and returns all parts, laid end to end along the dimension named above; an argument that names none is the same for every part. Nothing has to cross between parts.
All inputs are finite; a program needn't handle non-finite values.
Results may differ from a plain program's by a relative error of at most 0.00035.
Values sent between devices are 32-bit elements; how exact they have to be, the bound alone decides.
No kernel may reach another device: no remote copies, remote signals or barrier semaphores. Data moves between devices by JAX's collectives and lax.ppermute only.
A program may use at most 64 MiB of HBM per device.

v0:
```python
import math
import jax
import jax.numpy as jnp
from jax import lax
from jax.sharding import PartitionSpec as P

GROUPS = 32
ITERS = 2
TRAIN_STEPS = 1000
TIME = ("steps", "inner")


def noise_table():
    levels = jnp.arange(TRAIN_STEPS, dtype=jnp.float32)
    beta_values = 0.0001 + (0.02 - 0.0001) * levels / (TRAIN_STEPS - 1)
    return jnp.exp(jnp.cumsum(jnp.log1p(-beta_values)))


def lookup(table, levels):
    places = jnp.arange(TRAIN_STEPS, dtype=jnp.int32)
    return jnp.sum(jnp.where(places == levels[:, None], table, jnp.zeros_like(table)), axis=1)


def group_norm(hidden):
    times, patches, channels = hidden.shape

    def group_mean(values):
        per_channel = jnp.mean(values, axis=1).reshape(times, GROUPS, channels // GROUPS)
        per_group = jnp.mean(per_channel, axis=2, keepdims=True)
        return jnp.broadcast_to(per_group, per_channel.shape).reshape(times, 1, channels)

    offset = hidden - group_mean(hidden)
    return offset * lax.rsqrt(group_mean(offset * offset) + 1e-05)


def project(values, weight):
    return lax.dot_general(
        values.astype(jnp.bfloat16),
        weight,
        (((2,), (0,)), ((), ())),
        preferred_element_type=jnp.float32,
    )


def predict_noise(states, modulation, input_weight, first_weight, second_weight, output_weight):
    channels = input_weight.shape[1]
    scale_part = modulation[:, None, :channels]
    shift_part = modulation[:, None, channels:]
    entry = project(states, input_weight)
    act_one = jax.nn.silu(group_norm(entry) * (1.0 + scale_part) + shift_part)
    act_two = jax.nn.silu(group_norm(project(act_one, first_weight)))
    block = entry + project(act_two, second_weight)
    return project(jax.nn.silu(group_norm(block)), output_weight)


def shift_blocks(part, count, width, blocks):
    pairs = [(place, place + blocks * width) for place in range(count - blocks * width)]
    return lax.ppermute(part, TIME, pairs)


def earlier_blocks(part, count, width):
    total = shift_blocks(part, count, width, 1)
    reach = 1
    while reach < count // width - 1:
        total = total + shift_blocks(total, count, width, reach)
        reach *= 2
    return total


def shards(
    start_state,
    noise_draws,
    step_gaps,
    window_start,
    input_weight,
    embed_weight,
    first_weight,
    second_weight,
    output_weight,
):
    count = lax.axis_size(TIME)
    width = start_state.shape[0]
    assert count % width == 0
    groups = [list(range(first, first + width)) for first in range(0, count, width)]
    place = lax.axis_index(TIME)
    image = place % width
    first_time = place - image

    def exchange(values):
        return lax.all_to_all(values, TIME, 0, 0, axis_index_groups=groups, tiled=True)

    noise = exchange(noise_draws[0])
    later = jnp.arange(count + 1, dtype=jnp.int32) > place
    before = lax.psum(jnp.where(later, step_gaps[0], 0), TIME)
    marks = window_start[0] - lax.dynamic_slice_in_dim(before, first_time, width + 1)
    bars = lookup(noise_table(), marks)
    bar_now = bars[:-1, None, None]
    bar_next = bars[1:, None, None]
    half = embed_weight.shape[0] // 2
    frequency = jnp.exp(-math.log(10000.0) * jnp.arange(half, dtype=jnp.float32) / half)
    angles = marks[:-1, None].astype(jnp.float32) * frequency
    features = jnp.concatenate([jnp.cos(angles), jnp.sin(angles)], axis=1).astype(jnp.bfloat16)
    modulation = jnp.dot(features, embed_weight, preferred_element_type=jnp.float32)
    sigma = jnp.sqrt((1.0 - bar_next) / (1.0 - bar_now) * (1.0 - bar_now / bar_next))
    noise_coef = (1.0 - bar_next) * jnp.sqrt(bar_now / (bar_next * (1.0 - bar_now)))
    own = lax.dynamic_index_in_dim(start_state, image, 0, True)
    states = own
    for iteration in range(ITERS):
        predicted = predict_noise(
            states, modulation, input_weight, first_weight, second_weight, output_weight
        )
        clean = jnp.clip(
            (states - jnp.sqrt(1.0 - bar_now) * predicted) / jnp.sqrt(bar_now), -1.0, 1.0
        )
        implied = (states - jnp.sqrt(bar_now) * clean) / jnp.sqrt(1.0 - bar_now)
        drift = jnp.sqrt(bar_next) * clean + noise_coef * implied + sigma * noise - states
        totals = jnp.cumsum(drift, axis=0)
        base = own + earlier_blocks(totals[-1:], count, width)
        states = base + (totals - drift)
    return exchange(states + drift)[None]


def solution(mesh):
    return jax.shard_map(
        shards,
        mesh=mesh,
        in_specs=(
            P("groups", None, None),
            P(("groups", "steps", "inner"), None, None, None),
            P(("groups", "steps", "inner")),
            P("groups"),
            P(),
            P(),
            P(),
            P(),
            P(),
        ),
        out_specs=P(("groups", "steps", "inner"), None, None, None),
        check_vma=False,
    )
```

profile of v0, /device:TPU:0, one launch (start us, length us, event | category | flops | bytes accessed | tf_op | source)
XLA Modules:
  0.0 87.1 jit_solution(368406443984099906)
XLA Ops:
  0.0 5.4 %all-to-all-start = ((f32[8,32,768]{2,1,0:T(8,128)}), f32[8,32,768]{2,1,0:T(8,128)}, u32[]{:S(2)}, u32[]{:S(2)}) async-start(f32[8,32,768]{2,1,0:T(8,128)} %bitcast.78), calls=%async_computation | async-start | bytes 1572864 | tf_op jit(solution)/shard_map/all_to_all | solution.py:90
  6.8 18.0 %psum.7 = s32[17]{0:T(128)S(1)} all-reduce(s32[17]{0:T(128)S(1)} %compare_select_fusion), channel_id=1, replica_groups=mesh['groups'=2,'steps'=8,'inner'=2] {'steps','inner'}, use_global_device_ids=true, to_apply=%region_0.1 | all-reduce | flops 17 | bytes 136 | tf_op jit(solution)/shard_map/psum | solution.py:94
  25.4 1.5 %fusion.75 = f32[8,2048]{1,0:T(8,128)S(1)} fusion(bf16[256,2048]{1,0:T(8,128)(2,1)} %param.14, bf16[8,128]{1,0:T(8,128)(2,1)S(1)} %get-tuple-element.8, bf16[8,128]{1,0:T(8,128)(2,1)S(1)} %get-tuple-element.7), kind=kOutput, calls=%fused_computation.87 | convolution fusion | flops 8396800 | bytes 1118208 | tf_op jit(solution)/shard_map/dot_general | solution.py:103
  26.8 1.9 %fusion.88 = (f32[1024]{0:T(1024)S(1)}, f32[32,1024]{1,0:T(8,128)S(1)}) fusion(bf16[768,1024]{1,0:T(8,128)(2,1)} %param.13, f32[8,32,768]{2,1,0:T(8,128)} %param.9, s32[]{:T(128)S(6)} %select_n.23), kind=kOutput, calls=%fused_computation.128 | convolution fusion | flops 50363392 | bytes 1757188 | tf_op jit(solution)/shard_map/dot_general | solution.py:37
  29.5 0.8 fusion.89
  31.4 2.7 %fusion.90 = (f32[8,1024]{1,0:T(8,128)S(1)}, f32[8,32,1024]{2,1,0:T(8,128)S(1)}) fusion(bf16[1024,1024]{1,0:T(8,128)(2,1)} %param.16, f32[8,32,1024]{2,1,0:T(8,128)} %copy-done.5, f32[8,1024]{1,0:T(8,128)S(1)} %rsqrt.75, f32[8,1024]{1,0:T(8,128)S(1)} %sub.131, f32[32,1024]{1,0:T(8,128)S(1)} %get-tuple-element.15), kind=kOutput, calls=%fused_computation.130 | convolution fusion | flops 539222016 | bytes 4423680 | tf_op jit(solution)/shard_map/dot_general | solution.py:37
  35.6 0.9 %dynamic-slice_bitcast_fusion = f32[32,768]{1,0:T(8,128)S(1)} fusion(f32[8,32,768]{2,1,0:T(8,128)} %param.9, s32[]{:T(128)S(6)} %select_n.23), kind=kLoop, calls=%fused_computation.66 | loop fusion | bytes 196612 | tf_op jit(solution)/shard_map/sub | solution.py:113
  36.6 2.5 %add_subtract_fusion.1 = f32[8,32,768]{2,1,0:T(8,128)S(1)} fusion(bf16[1024,768]{1,0:T(8,128)(2,1)} %param.17, f32[8,32,768]{2,1,0:T(8,128)} %all-to-all-done, f32[8,32,1024]{2,1,0:T(8,128)S(1)} %get-tuple-element.19, f32[8,1024]{1,0:T(8,128)S(1)} %rsqrt.77, f32[8,1024]{1,0:T(8,128)S(1)} %sub.134, f32[8]{0:T(128)S(1)} %get-tuple-element.11, ...), kind=kOutput, calls=%fused_computation.38 | convolution fusion | flops 407044096 | bytes 4358304 | tf_op jit(solution)/shard_map/dot_general | solution.py:37
  39.1 1.7 %fusion.94 = f32[8,32,768]{2,1,0:T(8,128)S(1)} fusion(f32[8,32,768]{2,1,0:T(8,128)S(1)} %add_subtract_fusion.1), kind=kOutput, calls=%fused_computation.134 | output fusion | flops 1376256 | bytes 1572864 | tf_op jit(solution)/shard_map/jit(cumsum)/reduce_window_sum | solution.py:117
  40.8 1.9 %collective-permute-start = (f32[1,32,768]{2,1,0:T(8,128)S(1)}, f32[1,32,768]{2,1,0:T(8,128)S(1)}, u32[]{:S(2)}, u32[]{:S(2)}) collective-permute-start(f32[1,32,768]{2,1,0:T(8,128)S(1)} %slice.46), channel_id=1, source_target_pairs={{0,8},{1,9},{2,10},{3,11},{4,12},{5,13},{6,14},{7,15},{16,24},{17,... | collective-permute-start | bytes 294920 | tf_op jit(solution)/shard_map/ppermute | solution.py:58
  42.7 2.2 %collective-permute-done = f32[1,32,768]{2,1,0:T(8,128)S(1)} collective-permute-done((f32[1,32,768]{2,1,0:T(8,128)S(1)}, f32[1,32,768]{2,1,0:T(8,128)S(1)}, u32[]{:S(2)}, u32[]{:S(2)}) %collective-permute-start) | collective-permute-done | bytes 98336 | tf_op jit(solution)/shard_map/ppermute | solution.py:58
  44.9 0.9 %add_bitcast_fusion.1 = f32[32,768]{1,0:T(8,128)S(1)} fusion(f32[1,32,768]{2,1,0:T(8,128)S(1)} %collective-permute-done, f32[8,32,768]{2,1,0:T(8,128)} %param.9, s32[]{:T(128)S(6)} %select_n.23), kind=kLoop, calls=%fused_computation.64 | loop fusion | flops 24576 | bytes 294916 | tf_op jit(solution)/shard_map/add | solution.py:119
  45.8 0.6 fusion.91
  47.5 1.9 %fusion.92 = (f32[8,1024]{1,0:T(8,128)S(1)}, f32[8,32,1024]{2,1,0:T(8,128)}) fusion(bf16[1024,1024]{1,0:T(8,128)(2,1)S(1)} %copy-done, f32[8,32,1024]{2,1,0:T(8,128)S(1)} %get-tuple-element.21, f32[8,1024]{1,0:T(8,128)S(1)} %rsqrt.79, f32[8,1024]{1,0:T(8,128)S(1)} %sub.143, f32[8,1024]{1,0:T(8,128)S(1)} %get-tuple-element.6, ...), kind=kOutput, calls=%fused_computation.132 | convolution fusion | flops 539484160 | bytes 4358144 | tf_op jit(solution)/shard_map/dot_general | solution.py:37
  49.8 1.4 %multiply_reduce_fusion.1 = f32[8,1024]{1,0:T(8,128)S(1)} fusion(f32[8,32,1024]{2,1,0:T(8,128)} %get-tuple-element.23, f32[8,1024]{1,0:T(8,128)S(1)} %sub.146), kind=kLoop, calls=%fused_computation.27 | loop fusion | flops 778240 | bytes 1114112 | tf_op jit(solution)/shard_map/reduce_sum | solution.py:28
  51.7 3.7 %fusion.93 = (f32[8,1024]{1,0:T(8,128)S(1)}, f32[8,32,1024]{2,1,0:T(8,128)}) fusion(f32[8,32,1024]{2,1,0:T(8,128)S(1)} %get-tuple-element.21, bf16[1024,1024]{1,0:T(8,128)(2,1)} %param.16, f32[8,32,1024]{2,1,0:T(8,128)} %get-tuple-element.23, f32[8,1024]{1,0:T(8,128)S(1)} %rsqrt.81, f32[8,1024]{1,0:T(8,128)S(1)} %sub.146), kind=kOutput, calls=%fused_computation.133 | convolution fusion | flops 539222016 | bytes 5341184 | tf_op jit(solution)/shard_map/dot_general | solution.py:37
  55.8 1.4 %multiply_reduce_fusion = f32[8,1024]{1,0:T(8,128)S(1)} fusion(f32[8,32,1024]{2,1,0:T(8,128)} %get-tuple-element.25, f32[8,1024]{1,0:T(8,128)S(1)} %sub.149), kind=kLoop, calls=%fused_computation.25 | loop fusion | flops 778240 | bytes 1114112 | tf_op jit(solution)/shard_map/reduce_sum | solution.py:28
  57.7 3.1 %add_subtract_fusion = f32[8,32,768]{2,1,0:T(8,128)S(1)} fusion(bf16[1024,768]{1,0:T(8,128)(2,1)} %param.17, f32[8,32,768]{2,1,0:T(8,128)} %all-to-all-done, f32[8,32,1024]{2,1,0:T(8,128)} %get-tuple-element.25, f32[8,1024]{1,0:T(8,128)S(1)} %rsqrt.83, f32[8,1024]{1,0:T(8,128)S(1)} %sub.149, f32[8]{0:T(128)S(1)} %get-tuple-element.11, ...), kind=kOutput, calls=%fused_computation.36 | convolution fusion | flops 407437312 | bytes 5931168 | tf_op jit(solution)/shard_map/dot_general | solution.py:37
  60.7 1.7 %fusion.95 = f32[8,32,768]{2,1,0:T(8,128)S(1)} fusion(f32[8,32,768]{2,1,0:T(8,128)S(1)} %add_subtract_fusion), kind=kOutput, calls=%fused_computation.135 | output fusion | flops 1376256 | bytes 1572864 | tf_op jit(solution)/shard_map/jit(cumsum)/reduce_window_sum | solution.py:117
  62.4 5.3 %collective-permute-start.1 = (f32[1,32,768]{2,1,0:T(8,128)S(1)}, f32[1,32,768]{2,1,0:T(8,128)S(1)}, u32[]{:S(2)}, u32[]{:S(2)}) collective-permute-start(f32[1,32,768]{2,1,0:T(8,128)S(1)} %slice.47), channel_id=1, source_target_pairs={{0,8},{1,9},{2,10},{3,11},{4,12},{5,13},{6,14},{7,15},{16,24},{17,... | collective-permute-start | bytes 294920 | tf_op jit(solution)/shard_map/ppermute | solution.py:58
  67.8 2.2 %collective-permute-done.1 = f32[1,32,768]{2,1,0:T(8,128)S(1)} collective-permute-done((f32[1,32,768]{2,1,0:T(8,128)S(1)}, f32[1,32,768]{2,1,0:T(8,128)S(1)}, u32[]{:S(2)}, u32[]{:S(2)}) %collective-permute-start.1) | collective-permute-done | bytes 98336 | tf_op jit(solution)/shard_map/ppermute | solution.py:58
  69.9 0.9 %add_bitcast_fusion = f32[32,768]{1,0:T(8,128)S(1)} fusion(f32[1,32,768]{2,1,0:T(8,128)S(1)} %collective-permute-done.1, f32[8,32,768]{2,1,0:T(8,128)} %param.9, s32[]{:T(128)S(6)} %select_n.23), kind=kLoop, calls=%fused_computation.63 | loop fusion | flops 24576 | bytes 294916 | tf_op jit(solution)/shard_map/add | solution.py:119
  71.0 15.3 %all_to_all.10 = f32[8,32,768]{2,1,0:T(8,128)S(1)} all-to-all(f32[8,32,768]{2,1,0:T(8,128)S(1)} %add_add_fusion), channel_id=1, replica_groups={{0,1,2,3,4,5,6,7},{8,9,10,11,12,13,14,15},{16,17,18,19,20,21,22,23},{24..., dimensions={0} | all-to-all | bytes 1572864 | tf_op jit(solution)/shard_map/all_to_all | solution.py:90
  86.3 0.9 %copy.13 = f32[1,8,32,768]{3,2,1,0:T(8,128)} copy(f32[1,8,32,768]{3,2,1,0:T(8,128)S(1)} %bitcast.77) | data formatting | bytes 1572864
  (109 shorter events, 6.6 us)
Async XLA Ops:
  0.0 29.5 %copy-start = (bf16[1024,1024]{1,0:T(8,128)(2,1)S(1)}, bf16[1024,1024]{1,0:T(8,128)(2,1)}, u32[]{:S(2)}) copy-start(bf16[1024,1024]{1,0:T(8,128)(2,1)} %param.15) | copy-start | bytes 6291460
  0.0 36.6 %all-to-all-start = ((f32[8,32,768]{2,1,0:T(8,128)}), f32[8,32,768]{2,1,0:T(8,128)}, u32[]{:S(2)}, u32[]{:S(2)}) async-start(f32[8,32,768]{2,1,0:T(8,128)} %bitcast.78), calls=%async_computation | async-start | bytes 1572864 | tf_op jit(solution)/shard_map/all_to_all | solution.py:90
  30.3 1.0 %copy-start.5 = (f32[8,32,1024]{2,1,0:T(8,128)}, f32[8,32,1024]{2,1,0:T(8,128)S(1)}, u32[]{:S(2)}) copy-start(f32[8,32,1024]{2,1,0:T(8,128)S(1)} %get-tuple-element.17) | copy-start | bytes 3145732
  39.0 7.4 %copy-start.4 = (f32[8,32,768]{2,1,0:T(8,128)}, f32[8,32,768]{2,1,0:T(8,128)S(1)}, u32[]{:S(2)}) copy-start(f32[8,32,768]{2,1,0:T(8,128)S(1)} %add_subtract_fusion.1) | copy-start | bytes 2359300
  39.1 6.8 %copy-start.1 = (bf16[768,1024]{1,0:T(8,128)(2,1)S(1)}, bf16[768,1024]{1,0:T(8,128)(2,1)}, u32[]{:S(2)}) copy-start(bf16[768,1024]{1,0:T(8,128)(2,1)} %param.13) | copy-start | bytes 4718596
  40.8 5.7 %copy-start.2 = (f32[8,32,768]{2,1,0:T(8,128)}, f32[8,32,768]{2,1,0:T(8,128)S(1)}, u32[]{:S(2)}) copy-start(f32[8,32,768]{2,1,0:T(8,128)S(1)} %fusion.94) | copy-start | bytes 2359300
  40.8 4.1 %collective-permute-start = (f32[1,32,768]{2,1,0:T(8,128)S(1)}, f32[1,32,768]{2,1,0:T(8,128)S(1)}, u32[]{:S(2)}, u32[]{:S(2)}) collective-permute-start(f32[1,32,768]{2,1,0:T(8,128)S(1)} %slice.46), channel_id=1, source_target_pairs={{0,8},{1,9},{2,10},{3,11},{4,12},{5,13},{6,14},{7,15},{16,24},{17,... | collective-permute-start | bytes 294920 | tf_op jit(solution)/shard_map/ppermute | solution.py:58
  55.4 2.3 %copy-start.3 = (f32[8,32,768]{2,1,0:T(8,128)S(1)}, f32[8,32,768]{2,1,0:T(8,128)}, u32[]{:S(2)}) copy-start(f32[8,32,768]{2,1,0:T(8,128)} %copy-done.2) | copy-start | bytes 2359300
  62.4 7.5 %collective-permute-start.1 = (f32[1,32,768]{2,1,0:T(8,128)S(1)}, f32[1,32,768]{2,1,0:T(8,128)S(1)}, u32[]{:S(2)}, u32[]{:S(2)}) collective-permute-start(f32[1,32,768]{2,1,0:T(8,128)S(1)} %slice.47), channel_id=1, source_target_pairs={{0,8},{1,9},{2,10},{3,11},{4,12},{5,13},{6,14},{7,15},{16,24},{17,... | collective-permute-start | bytes 294920 | tf_op jit(solution)/shard_map/ppermute | solution.py:58
where the time goes:
time: 87.7 us; the launch traced here: 87.1 us
  blocking collectives  33.3 us (38%)
  matrix products  18.5 us (21%)
  starting transfers between devices  12.6 us (14%)
  other arithmetic  11 us (13%)
  local copies, waits for them, and re-layouts  5.39 us (6%)
  waiting for transfers between devices  4.38 us (5%)
  between operations  1.9 us (2%)
    psum x1, blocking collectives, shards(): before = lax.psum(jnp.where(later, step_gaps[0], 0), TIME)  18 us
    dot_general x8, matrix products, project(): lax.dot_general(values.astype(jnp.bfloat16), weight, (((2,), (0,)), ((),...  17.1 us
    all_to_all x1, blocking collectives, exchange(): lax.all_to_all(values, TIME, 0, 0, axis_index_groups=groups, tiled=True)  15.3 us
    ppermute x2, starting transfers between devices, shift_blocks(): return lax.ppermute(part, TIME, pairs)  7.21 us
    all_to_all x1, starting transfers between devices, exchange(): lax.all_to_all(values, TIME, 0, 0, axis_index_groups=groups, tiled=True)  5.42 us
    ppermute x2, waiting for transfers between devices, shift_blocks(): return lax.ppermute(part, TIME, pairs)  4.38 us
    another operation x2, other arithmetic, shards(): totals = jnp.cumsum(drift, axis=0)  3.39 us
    reduce_sum x6, other arithmetic, group_mean(): jnp.mean(values, axis=1).reshape(times, GROUPS, channels // GROUPS)  3.38 us
  transfers between devices with their start and end apart: 3, of which 2 were waited for; matrix products, arithmetic and copies ran while one was open for 13% of the time, Pallas kernels for 0%

commit v1 on v0

--- a/solution.py
+++ b/solution.py
@@ -91,7 +91,7 @@
 
     noise = exchange(noise_draws[0])
     later = jnp.arange(count + 1, dtype=jnp.int32) > place
-    before = lax.psum(jnp.where(later, step_gaps[0], 0), TIME)
+    before = jnp.sum(lax.all_gather(jnp.where(later, step_gaps[0], 0), TIME), axis=0)
     marks = window_start[0] - lax.dynamic_slice_in_dim(before, first_time, width + 1)
     bars = lookup(noise_table(), marks)
     bar_now = bars[:-1, None, None]

time: 87.7 us -> 95.7 us (1.091)
  blocking collectives: 33.3 us -> 41.2 us
    all_gather x0 -> x1, blocking collectives: none -> 24 us  [shards(): lax.all_gather(jnp.where(later, step_gaps[0], 0), TIME)]
    psum x1 -> x0, blocking collectives: 18 us -> none  [shards(): before = lax.psum(jnp.where(later, step_gaps[0], 0), TIME)]
    all_to_all x1, blocking collectives: 15.3 us -> 17.2 us  [exchange(): lax.all_to_all(values, TIME, 0, 0, axis_index_groups=groups, tiled=True)]
  transfers between devices with their start and end apart: 3 -> 3, of which waited for: 2 -> 2; matrix products, arithmetic and copies ran while one was open for 13% -> 12% of each run, Pallas kernels for 0% -> 0%
where the time goes in v1:
time: 95.7 us; the launch traced here: 95.2 us
  blocking collectives  41.2 us (43%)
  matrix products  18.5 us (19%)
  starting transfers between devices  12.1 us (13%)
  other arithmetic  11.1 us (12%)
  local copies, waits for them, and re-layouts  5.39 us (6%)
  waiting for transfers between devices  5.05 us (5%)
  between operations  1.91 us (2%)
    all_gather x1, blocking collectives, shards(): lax.all_gather(jnp.where(later, step_gaps[0], 0), TIME)  24 us
    all_to_all x1, blocking collectives, exchange(): lax.all_to_all(values, TIME, 0, 0, axis_index_groups=groups, tiled=True)  17.2 us
    dot_general x8, matrix products, project(): lax.dot_general(values.astype(jnp.bfloat16), weight, (((2,), (0,)), ((),...  17 us
    ppermute x2, starting transfers between devices, shift_blocks(): return lax.ppermute(part, TIME, pairs)  6.66 us
    all_to_all x1, starting transfers between devices, exchange(): lax.all_to_all(values, TIME, 0, 0, axis_index_groups=groups, tiled=True)  5.42 us
    ppermute x2, waiting for transfers between devices, shift_blocks(): return lax.ppermute(part, TIME, pairs)  5.04 us
    another operation x2, other arithmetic, shards(): totals = jnp.cumsum(drift, axis=0)  3.39 us
    reduce_sum x6, other arithmetic, group_mean(): jnp.mean(values, axis=1).reshape(times, GROUPS, channels // GROUPS)  3.38 us
  transfers between devices with their start and end apart: 3, of which 2 were waited for; matrix products, arithmetic and copies ran while one was open for 12% of the time, Pallas kernels for 0%

profile of v1, /device:TPU:0, one launch (start us, length us, event | category | flops | bytes accessed | tf_op | source)
XLA Modules:
  0.0 95.2 jit_solution(16028556573466421383)
XLA Ops:
  0.0 5.4 %all-to-all-start = ((f32[8,32,768]{2,1,0:T(8,128)}), f32[8,32,768]{2,1,0:T(8,128)}, u32[]{:S(2)}, u32[]{:S(2)}) async-start(f32[8,32,768]{2,1,0:T(8,128)} %bitcast.80), calls=%async_computation | async-start | bytes 1572864 | tf_op jit(solution)/shard_map/all_to_all | solution.py:90
  7.2 24.0 %all-gather = s32[16,1,17]{2,1,0:T(1,128)S(1)} all-gather(s32[1,1,17]{2,1,0:T(1,128)S(1)} %fusion.79), channel_id=1, replica_groups=mesh['groups'=2,'steps'=8,'inner'=2] {'steps','inner'}, dimensions={0}, use_global_device_ids=true | all-gather | bytes 1156 | tf_op jit(solution)/shard_map/all_gather | solution.py:94
  31.4 1.5 %fusion.75 = f32[8,2048]{1,0:T(8,128)S(1)} fusion(bf16[256,2048]{1,0:T(8,128)(2,1)} %param.14, bf16[8,128]{1,0:T(8,128)(2,1)S(1)} %get-tuple-element.8, bf16[8,128]{1,0:T(8,128)(2,1)S(1)} %get-tuple-element.7), kind=kOutput, calls=%fused_computation.87 | convolution fusion | flops 8396800 | bytes 1118208 | tf_op jit(solution)/shard_map/dot_general | solution.py:103
  32.9 1.9 %fusion.89 = (f32[1024]{0:T(1024)S(1)}, f32[32,1024]{1,0:T(8,128)S(1)}) fusion(bf16[768,1024]{1,0:T(8,128)(2,1)} %param.13, f32[8,32,768]{2,1,0:T(8,128)} %param.9, s32[]{:T(128)S(6)} %select_n.30), kind=kOutput, calls=%fused_computation.129 | convolution fusion | flops 50363392 | bytes 1757188 | tf_op jit(solution)/shard_map/dot_general | solution.py:37
  35.5 0.8 fusion.90
  37.4 2.7 %fusion.91 = (f32[8,1024]{1,0:T(8,128)S(1)}, f32[8,32,1024]{2,1,0:T(8,128)S(1)}) fusion(bf16[1024,1024]{1,0:T(8,128)(2,1)} %param.16, f32[8,32,1024]{2,1,0:T(8,128)} %copy-done.5, f32[8,1024]{1,0:T(8,128)S(1)} %rsqrt.75, f32[8,1024]{1,0:T(8,128)S(1)} %sub.131, f32[32,1024]{1,0:T(8,128)S(1)} %get-tuple-element.15), kind=kOutput, calls=%fused_computation.131 | convolution fusion | flops 539222016 | bytes 4423680 | tf_op jit(solution)/shard_map/dot_general | solution.py:37
  41.6 0.9 dynamic-slice_bitcast_fusion
  42.6 2.5 %add_subtract_fusion.1 = f32[8,32,768]{2,1,0:T(8,128)S(1)} fusion(bf16[1024,768]{1,0:T(8,128)(2,1)} %param.17, f32[8,32,768]{2,1,0:T(8,128)} %all-to-all-done, f32[8,32,1024]{2,1,0:T(8,128)S(1)} %get-tuple-element.19, f32[8,1024]{1,0:T(8,128)S(1)} %rsqrt.77, f32[8,1024]{1,0:T(8,128)S(1)} %sub.134, f32[8]{0:T(128)S(1)} %get-tuple-element.11, ...), kind=kOutput, calls=%fused_computation.38 | convolution fusion | flops 407044096 | bytes 4358304 | tf_op jit(solution)/shard_map/dot_general | solution.py:37
  45.1 1.7 %fusion.95 = f32[8,32,768]{2,1,0:T(8,128)S(1)} fusion(f32[8,32,768]{2,1,0:T(8,128)S(1)} %add_subtract_fusion.1), kind=kOutput, calls=%fused_computation.135 | output fusion | flops 1376256 | bytes 1572864 | tf_op jit(solution)/shard_map/jit(cumsum)/reduce_window_sum | solution.py:117
  46.8 1.3 %collective-permute-start = (f32[1,32,768]{2,1,0:T(8,128)S(1)}, f32[1,32,768]{2,1,0:T(8,128)S(1)}, u32[]{:S(2)}, u32[]{:S(2)}) collective-permute-start(f32[1,32,768]{2,1,0:T(8,128)S(1)} %slice.46), channel_id=1, source_target_pairs={{0,8},{1,9},{2,10},{3,11},{4,12},{5,13},{6,14},{7,15},{16,24},{17,... | collective-permute-start | bytes 294920 | tf_op jit(solution)/shard_map/ppermute | solution.py:58
  48.1 2.9 %collective-permute-done = f32[1,32,768]{2,1,0:T(8,128)S(1)} collective-permute-done((f32[1,32,768]{2,1,0:T(8,128)S(1)}, f32[1,32,768]{2,1,0:T(8,128)S(1)}, u32[]{:S(2)}, u32[]{:S(2)}) %collective-permute-start) | collective-permute-done | bytes 98336 | tf_op jit(solution)/shard_map/ppermute | solution.py:58
  51.0 0.9 add_bitcast_fusion.1
  51.9 0.6 fusion.92
  53.6 1.9 %fusion.93 = (f32[8,1024]{1,0:T(8,128)S(1)}, f32[8,32,1024]{2,1,0:T(8,128)}) fusion(bf16[1024,1024]{1,0:T(8,128)(2,1)S(1)} %copy-done, f32[8,32,1024]{2,1,0:T(8,128)S(1)} %get-tuple-element.21, f32[8,1024]{1,0:T(8,128)S(1)} %rsqrt.79, f32[8,1024]{1,0:T(8,128)S(1)} %sub.143, f32[8,1024]{1,0:T(8,128)S(1)} %get-tuple-element.6, ...), kind=kOutput, calls=%fused_computation.133 | convolution fusion | flops 539484160 | bytes 4358144 | tf_op jit(solution)/shard_map/dot_general | solution.py:37
  55.9 1.4 %multiply_reduce_fusion.1 = f32[8,1024]{1,0:T(8,128)S(1)} fusion(f32[8,32,1024]{2,1,0:T(8,128)} %get-tuple-element.23, f32[8,1024]{1,0:T(8,128)S(1)} %sub.146), kind=kLoop, calls=%fused_computation.27 | loop fusion | flops 778240 | bytes 1114112 | tf_op jit(solution)/shard_map/reduce_sum | solution.py:28
  57.8 3.7 %fusion.94 = (f32[8,1024]{1,0:T(8,128)S(1)}, f32[8,32,1024]{2,1,0:T(8,128)}) fusion(f32[8,32,1024]{2,1,0:T(8,128)S(1)} %get-tuple-element.21, bf16[1024,1024]{1,0:T(8,128)(2,1)} %param.16, f32[8,32,1024]{2,1,0:T(8,128)} %get-tuple-element.23, f32[8,1024]{1,0:T(8,128)S(1)} %rsqrt.81, f32[8,1024]{1,0:T(8,128)S(1)} %sub.146), kind=kOutput, calls=%fused_computation.134 | convolution fusion | flops 539222016 | bytes 5341184 | tf_op jit(solution)/shard_map/dot_general | solution.py:37
  61.9 1.4 %multiply_reduce_fusion = f32[8,1024]{1,0:T(8,128)S(1)} fusion(f32[8,32,1024]{2,1,0:T(8,128)} %get-tuple-element.25, f32[8,1024]{1,0:T(8,128)S(1)} %sub.149), kind=kLoop, calls=%fused_computation.25 | loop fusion | flops 778240 | bytes 1114112 | tf_op jit(solution)/shard_map/reduce_sum | solution.py:28
  63.7 3.1 %add_subtract_fusion = f32[8,32,768]{2,1,0:T(8,128)S(1)} fusion(bf16[1024,768]{1,0:T(8,128)(2,1)} %param.17, f32[8,32,768]{2,1,0:T(8,128)} %all-to-all-done, f32[8,32,1024]{2,1,0:T(8,128)} %get-tuple-element.25, f32[8,1024]{1,0:T(8,128)S(1)} %rsqrt.83, f32[8,1024]{1,0:T(8,128)S(1)} %sub.149, f32[8]{0:T(128)S(1)} %get-tuple-element.11, ...), kind=kOutput, calls=%fused_computation.36 | convolution fusion | flops 407437312 | bytes 5931168 | tf_op jit(solution)/shard_map/dot_general | solution.py:37
  66.8 1.7 %fusion.96 = f32[8,32,768]{2,1,0:T(8,128)S(1)} fusion(f32[8,32,768]{2,1,0:T(8,128)S(1)} %add_subtract_fusion), kind=kOutput, calls=%fused_computation.136 | output fusion | flops 1376256 | bytes 1572864 | tf_op jit(solution)/shard_map/jit(cumsum)/reduce_window_sum | solution.py:117
  68.5 5.4 %collective-permute-start.1 = (f32[1,32,768]{2,1,0:T(8,128)S(1)}, f32[1,32,768]{2,1,0:T(8,128)S(1)}, u32[]{:S(2)}, u32[]{:S(2)}) collective-permute-start(f32[1,32,768]{2,1,0:T(8,128)S(1)} %slice.47), channel_id=1, source_target_pairs={{0,8},{1,9},{2,10},{3,11},{4,12},{5,13},{6,14},{7,15},{16,24},{17,... | collective-permute-start | bytes 294920 | tf_op jit(solution)/shard_map/ppermute | solution.py:58
  73.9 2.2 %collective-permute-done.1 = f32[1,32,768]{2,1,0:T(8,128)S(1)} collective-permute-done((f32[1,32,768]{2,1,0:T(8,128)S(1)}, f32[1,32,768]{2,1,0:T(8,128)S(1)}, u32[]{:S(2)}, u32[]{:S(2)}) %collective-permute-start.1) | collective-permute-done | bytes 98336 | tf_op jit(solution)/shard_map/ppermute | solution.py:58
  76.1 0.9 add_bitcast_fusion
  77.1 17.2 %all_to_all.10 = f32[8,32,768]{2,1,0:T(8,128)S(1)} all-to-all(f32[8,32,768]{2,1,0:T(8,128)S(1)} %add_add_fusion), channel_id=1, replica_groups={{0,1,2,3,4,5,6,7},{8,9,10,11,12,13,14,15},{16,17,18,19,20,21,22,23},{24..., dimensions={0} | all-to-all | bytes 1572864 | tf_op jit(solution)/shard_map/all_to_all | solution.py:90
  94.3 0.9 copy.13
  (110 shorter events, 6.6 us)
Async XLA Ops:
  0.0 35.5 %copy-start = (bf16[1024,1024]{1,0:T(8,128)(2,1)S(1)}, bf16[1024,1024]{1,0:T(8,128)(2,1)}, u32[]{:S(2)}) copy-start(bf16[1024,1024]{1,0:T(8,128)(2,1)} %param.15) | copy-start | bytes 6291460
  0.0 42.6 %all-to-all-start = ((f32[8,32,768]{2,1,0:T(8,128)}), f32[8,32,768]{2,1,0:T(8,128)}, u32[]{:S(2)}, u32[]{:S(2)}) async-start(f32[8,32,768]{2,1,0:T(8,128)} %bitcast.80), calls=%async_computation | async-start | bytes 1572864 | tf_op jit(solution)/shard_map/all_to_all | solution.py:90
  36.3 1.0 %copy-start.5 = (f32[8,32,1024]{2,1,0:T(8,128)}, f32[8,32,1024]{2,1,0:T(8,128)S(1)}, u32[]{:S(2)}) copy-start(f32[8,32,1024]{2,1,0:T(8,128)S(1)} %get-tuple-element.17) | copy-start | bytes 3145732
  45.1 7.4 %copy-start.4 = (f32[8,32,768]{2,1,0:T(8,128)}, f32[8,32,768]{2,1,0:T(8,128)S(1)}, u32[]{:S(2)}) copy-start(f32[8,32,768]{2,1,0:T(8,128)S(1)} %add_subtract_fusion.1) | copy-start | bytes 2359300
  45.1 6.8 %copy-start.1 = (bf16[768,1024]{1,0:T(8,128)(2,1)S(1)}, bf16[768,1024]{1,0:T(8,128)(2,1)}, u32[]{:S(2)}) copy-start(bf16[768,1024]{1,0:T(8,128)(2,1)} %param.13) | copy-start | bytes 4718596
  46.8 5.7 %copy-start.2 = (f32[8,32,768]{2,1,0:T(8,128)}, f32[8,32,768]{2,1,0:T(8,128)S(1)}, u32[]{:S(2)}) copy-start(f32[8,32,768]{2,1,0:T(8,128)S(1)} %fusion.95) | copy-start | bytes 2359300
  46.8 4.2 %collective-permute-start = (f32[1,32,768]{2,1,0:T(8,128)S(1)}, f32[1,32,768]{2,1,0:T(8,128)S(1)}, u32[]{:S(2)}, u32[]{:S(2)}) collective-permute-start(f32[1,32,768]{2,1,0:T(8,128)S(1)} %slice.46), channel_id=1, source_target_pairs={{0,8},{1,9},{2,10},{3,11},{4,12},{5,13},{6,14},{7,15},{16,24},{17,... | collective-permute-start | bytes 294920 | tf_op jit(solution)/shard_map/ppermute | solution.py:58
  61.4 2.3 %copy-start.3 = (f32[8,32,768]{2,1,0:T(8,128)S(1)}, f32[8,32,768]{2,1,0:T(8,128)}, u32[]{:S(2)}) copy-start(f32[8,32,768]{2,1,0:T(8,128)} %copy-done.2) | copy-start | bytes 2359300
  68.5 7.6 %collective-permute-start.1 = (f32[1,32,768]{2,1,0:T(8,128)S(1)}, f32[1,32,768]{2,1,0:T(8,128)S(1)}, u32[]{:S(2)}, u32[]{:S(2)}) collective-permute-start(f32[1,32,768]{2,1,0:T(8,128)S(1)} %slice.47), channel_id=1, source_target_pairs={{0,8},{1,9},{2,10},{3,11},{4,12},{5,13},{6,14},{7,15},{16,24},{17,... | collective-permute-start | bytes 294920 | tf_op jit(solution)/shard_map/ppermute | solution.py:58
